TPU v7x, 32 devices: a whole 2x2x4 slice. The times are simulated.
32 devices in a mesh: row: 16 (over z, y, core), col: 2 (over x).
Axes of the slice: x: 2, y: 2, z: 4, core: 2. Of those that a mesh axis runs over, the one named last changes fastest.
Arguments:
- pair_rep: bfloat16 [2048, 2048, 128], P('row', 'col'), may hold values from -6 to 6
- bias_weight: bfloat16 [128, 12], replicated, may hold values from -0.5 to 0.5
- head_weight: float32 [12], replicated, may hold values from -1 to 1
- queries: float32 [192, 2048], P(None, 'row'), may hold values from -48 to 48, as said below
- key_vectors: float32 [192, 2048], P(None, 'col'), may hold values from -48 to 48, as said below
- values: float32 [192, 2048], P(None, 'col'), may hold values from -6 to 6
- query_points: float32 [3, 48, 2048], P(None, None, 'row'), may hold values from -6 to 6
- key_points: float32 [3, 48, 2048], P(None, None, 'col'), may hold values from -6 to 6
- value_points: float32 [3, 96, 2048], P(None, None, 'col'), may hold values from -6 to 6
- rotations: float32 [3, 3, 2048], replicated, may hold values from -1 to 1, as said below
- translations: float32 [3, 2048], replicated, may hold values from -12 to 12
- residue_count: int32 [1], replicated, may hold values from 1024 to 2048
- grad_output: float32 [192, 2048], P(None, 'row'), may hold values from -6 to 6
- grad_points: float32 [3, 96, 2048], P(None, None, 'row'), may hold values from -6 to 6
- grad_pair: bfloat16 [2048, 12, 128], P('row'), may hold values from -2 to 2
Outputs:
- pair_grad: bfloat16 [2048, 2048, 128], P('row', 'col')
- query_grad: float32 [192, 2048], P(None, ('row', 'col'))
- query_point_grad: float32 [3, 48, 2048], P(None, None, ('row', 'col'))
- query_frame_grad: float32 [3, 4, 2048], P(None, None, ('row', 'col'))
- key_grad: float32 [192, 2048], P(None, ('col', 'row'))
- value_grad: float32 [192, 2048], P(None, ('col', 'row'))
- key_point_grad: float32 [3, 48, 2048], P(None, None, ('col', 'row'))
- value_point_grad: float32 [3, 96, 2048], P(None, None, ('col', 'row'))
- key_frame_grad: float32 [3, 4, 2048], P(None, None, ('col', 'row'))
- bias_weight_grad: float32 [128, 12], replicated
- head_weight_grad: float32 [12], replicated
Inputs may be any that keep to these rules, and one draw needn't show every extreme that they name: `queries`: entries of order one, except a few residues whose vectors are much larger. `key_vectors`: entries of order one, except a few residues whose vectors are much larger. `rotations`: each residue's 3 x 3 matrix is a rotation: orthonormal with determinant one.
All inputs are finite; a program needn't handle non-finite values.
Results may differ from a plain program's by a relative error of at most 0.0049.
Values sent between devices are 32-bit elements; how exact they have to be, the bound alone decides.
A program may use at most 256 MiB of HBM per device.

v0:
```python
import math

import jax
import jax.numpy as jnp
from jax import lax
from jax.sharding import PartitionSpec as P

HIGHEST = lax.Precision.HIGHEST


def joined(value, axis, join):
    pieces = jax.tree.map(lambda part: lax.all_gather(part, axis), value)
    head = jax.tree.map(lambda part: part[0], pieces)
    tail = jax.tree.map(lambda part: part[1:], pieces)
    total, _ = lax.scan(lambda total, share: (join(total, share), None), head, tail)
    return total


def globalize(rotation, offset, local):
    return jnp.einsum("xym,ykm->xkm", rotation, local, precision=HIGHEST) + offset[:, None, :]


def rotate_back(rotation, vector):
    return jnp.einsum("xym,xkm->ykm", rotation, vector, precision=HIGHEST)


def frame_terms(grad_global, local):
    rotation_part = jnp.einsum("xkm,ykm->xym", grad_global, local, precision=HIGHEST)
    return jnp.concatenate([rotation_part, jnp.sum(grad_global, axis=1)[:, None, :]], axis=1)


def output_frame_terms(point_out, offset, cotan_local, grad_rotated):
    rotation_part = jnp.einsum(
        "xkm,ykm->xym", point_out - offset[:, None, :], cotan_local, precision=HIGHEST
    )
    return jnp.concatenate([rotation_part, -jnp.sum(grad_rotated, axis=1)[:, None, :]], axis=1)


def merge_stats(first, second):
    top = jnp.maximum(first[0], second[0])
    first_factor = jnp.exp(first[0] - top)
    second_factor = jnp.exp(second[0] - top)
    return (
        top,
        first[1] * first_factor + second[1] * second_factor,
        first[2] * first_factor + second[2] * second_factor,
        first[3] * first_factor[None, :, None, :] + second[3] * second_factor[None, :, None, :],
    )


def per_device(
    pair_rep,
    bias_weight,
    head_weight,
    queries,
    key_vectors,
    values,
    query_points,
    key_points,
    value_points,
    rotations,
    translations,
    residue_count,
    grad_output,
    grad_points,
    grad_pair,
):
    heads = bias_weight.shape[1]
    width = queries.shape[0] // heads
    qpoints = query_points.shape[1] // heads
    vpoints = value_points.shape[1] // heads
    rows_here = queries.shape[1]
    cols_here = key_vectors.shape[1]
    logit_scale = math.sqrt(1.0 / 3.0)
    point_scale = math.sqrt(2.0 / (9.0 * qpoints))
    inner_scale = 1.0 / math.sqrt(width)
    distance_coef = 0.5 * logit_scale * point_scale * jax.nn.softplus(head_weight)
    row_start = lax.axis_index("row") * rows_here
    col_start = lax.axis_index("col") * cols_here
    rot_rows = lax.dynamic_slice_in_dim(rotations, row_start, rows_here, 2)
    shift_rows = lax.dynamic_slice_in_dim(translations, row_start, rows_here, 1)
    rot_cols = lax.dynamic_slice_in_dim(rotations, col_start, cols_here, 2)
    shift_cols = lax.dynamic_slice_in_dim(translations, col_start, cols_here, 1)
    query_global = globalize(rot_rows, shift_rows, query_points).reshape(
        3, heads, qpoints, rows_here
    )
    key_global = globalize(rot_cols, shift_cols, key_points).reshape(3, heads, qpoints, cols_here)
    value_global = globalize(rot_cols, shift_cols, value_points).reshape(
        3, heads, vpoints, cols_here
    )
    grad_flat = jnp.einsum("xym,ykm->xkm", rot_rows, grad_points, precision=HIGHEST)
    grad_heads = grad_flat.reshape(3, heads, vpoints, rows_here)
    query_heads = queries.reshape(heads, width, rows_here)
    out_heads = grad_output.reshape(heads, width, rows_here)
    key_heads = key_vectors.reshape(heads, width, cols_here)
    value_heads = values.reshape(heads, width, cols_here)
    valid = col_start + lax.iota(jnp.int32, cols_here) < residue_count[0]
    inner = jnp.einsum("hci,hcj->hij", query_heads, key_heads, precision=HIGHEST)
    cross = jnp.einsum("xhpi,xhpj->hij", query_global, key_global, precision=HIGHEST)
    distance = (
        jnp.sum(query_global**2, axis=(0, 2))[:, :, None]
        + jnp.sum(key_global**2, axis=(0, 2))[:, None, :]
        - 2.0 * cross
    )
    bias = jnp.einsum("ijc,ch->hij", pair_rep, bias_weight, preferred_element_type=jnp.float32)
    logits = logit_scale * (inner_scale * inner + bias) - distance_coef[:, None, None] * distance
    logits = jnp.where(valid[None, None, :], logits, jnp.float32(-1000000000.0))
    product = (
        jnp.einsum("hci,hcj->hij", out_heads, value_heads, precision=HIGHEST)
        + jnp.einsum("xhvi,xhvj->hij", grad_heads, value_global, precision=HIGHEST)
        + jnp.einsum("ijc,ihc->hij", pair_rep, grad_pair, preferred_element_type=jnp.float32)
    )
    local_peak = jnp.max(logits, axis=2)
    exponent = jnp.exp(logits - local_peak[:, :, None])
    local_total = jnp.sum(exponent, axis=2)
    local_upper = jnp.sum(exponent * product, axis=2)
    local_points = jnp.einsum("hij,xhvj->xhvi", exponent, value_global, precision=HIGHEST)
    row_peak, row_total, row_upper, row_points = joined(
        (local_peak, local_total, local_upper, local_points), "col", merge_stats
    )
    attention = jnp.exp(logits - row_peak[:, :, None]) / row_total[:, :, None]
    delta = row_upper / row_total
    point_out = (row_points / row_total[None, :, None, :]).reshape(3, heads * vpoints, rows_here)
    logit_grad = attention * (product - delta[:, :, None])
    grad_rounded = logit_grad.astype(jnp.bfloat16)
    attn_rounded = attention.astype(jnp.bfloat16)
    pair_grad = (
        logit_scale
        * jnp.einsum("hij,ch->ijc", grad_rounded, bias_weight, preferred_element_type=jnp.float32)
        + jnp.einsum("hij,ihc->ijc", attn_rounded, grad_pair, preferred_element_type=jnp.float32)
    ).astype(jnp.bfloat16)
    weight_part = logit_scale * jnp.einsum(
        "ijc,hij->ch", pair_rep, grad_rounded, preferred_element_type=jnp.float32
    )
    distance_part = jnp.sum(logit_grad * distance, axis=(1, 2))
    query_part = (
        logit_scale
        * inner_scale
        * jnp.einsum("hij,hcj->hci", logit_grad, key_heads, precision=HIGHEST)
    )
    row_sum = jnp.sum(logit_grad, axis=2)
    qpoint_part = (
        -2.0
        * distance_coef[None, :, None, None]
        * (
            query_global * row_sum[None, :, None, :]
            - jnp.einsum("hij,xhpj->xhpi", logit_grad, key_global, precision=HIGHEST)
        )
    )
    query_grad, qpoint_sum = (
        lax.psum_scatter(
            query_part.reshape(heads * width, rows_here), "col", scatter_dimension=1, tiled=True
        ),
        lax.psum_scatter(
            qpoint_part.reshape(3, heads * qpoints, rows_here),
            "col",
            scatter_dimension=2,
            tiled=True,
        ),
    )
    share = rows_here // lax.axis_size("col")
    share_start = lax.axis_index("col") * share
    own_start = row_start + share_start
    rot_own = lax.dynamic_slice_in_dim(rotations, own_start, share, 2)
    shift_own = lax.dynamic_slice_in_dim(translations, own_start, share, 1)
    local_own = lax.dynamic_slice_in_dim(query_points, share_start, share, 2)
    cotan_own = lax.dynamic_slice_in_dim(grad_points, share_start, share, 2)
    out_own = lax.dynamic_slice_in_dim(point_out, share_start, share, 2)
    rotated_own = lax.dynamic_slice_in_dim(grad_flat, share_start, share, 2)
    query_point_grad = rotate_back(rot_own, qpoint_sum)
    query_frame_grad = frame_terms(qpoint_sum, local_own) + output_frame_terms(
        out_own, shift_own, cotan_own, rotated_own
    )
    key_part = (
        logit_scale
        * inner_scale
        * jnp.einsum("hij,hci->hcj", logit_grad, query_heads, precision=HIGHEST)
    )
    value_part = jnp.einsum("hij,hci->hcj", attention, out_heads, precision=HIGHEST)
    col_sum = jnp.sum(logit_grad, axis=1)
    kpoint_part = (
        2.0
        * distance_coef[None, :, None, None]
        * (
            jnp.einsum("hij,xhpi->xhpj", logit_grad, query_global, precision=HIGHEST)
            - key_global * col_sum[None, :, None, :]
        )
    ).reshape(3, heads * qpoints, cols_here)
    vpoint_part = jnp.einsum("hij,xhvi->xhvj", attention, grad_heads, precision=HIGHEST).reshape(
        3, heads * vpoints, cols_here
    )
    key_flat = key_part.reshape(heads * width, cols_here)
    value_flat = value_part.reshape(heads * width, cols_here)
    key_grad, value_grad, kpoint_sum, vpoint_sum = (
        lax.psum_scatter(key_flat, "row", scatter_dimension=1, tiled=True),
        lax.psum_scatter(value_flat, "row", scatter_dimension=1, tiled=True),
        lax.psum_scatter(kpoint_part, "row", scatter_dimension=2, tiled=True),
        lax.psum_scatter(vpoint_part, "row", scatter_dimension=2, tiled=True),
    )
    kshare = cols_here // lax.axis_size("row")
    kshare_start = lax.axis_index("row") * kshare
    rot_keys = lax.dynamic_slice_in_dim(rotations, col_start + kshare_start, kshare, 2)
    klocal_own = lax.dynamic_slice_in_dim(key_points, kshare_start, kshare, 2)
    vlocal_own = lax.dynamic_slice_in_dim(value_points, kshare_start, kshare, 2)
    key_point_grad = rotate_back(rot_keys, kpoint_sum)
    value_point_grad = rotate_back(rot_keys, vpoint_sum)
    key_frame_grad = frame_terms(kpoint_sum, klocal_own) + frame_terms(vpoint_sum, vlocal_own)
    weight_total, distance_total = lax.psum((weight_part, distance_part), ("row", "col"))
    head_weight_grad = (
        distance_total * (-0.5 * logit_scale * point_scale) * jax.nn.sigmoid(head_weight)
    )
    return (
        pair_grad,
        query_grad,
        query_point_grad,
        query_frame_grad,
        key_grad,
        value_grad,
        key_point_grad,
        value_point_grad,
        key_frame_grad,
        weight_total,
        head_weight_grad,
    )


def solution(mesh):
    return jax.shard_map(
        per_device,
        mesh=mesh,
        in_specs=(
            P("row", "col", None),
            P(),
            P(),
            P(None, "row"),
            P(None, "col"),
            P(None, "col"),
            P(None, None, "row"),
            P(None, None, "col"),
            P(None, None, "col"),
            P(),
            P(),
            P(),
            P(None, "row"),
            P(None, None, "row"),
            P("row", None, None),
        ),
        out_specs=(
            P("row", "col", None),
            P(None, ("row", "col")),
            P(None, None, ("row", "col")),
            P(None, None, ("row", "col")),
            P(None, ("col", "row")),
            P(None, ("col", "row")),
            P(None, None, ("col", "row")),
            P(None, None, ("col", "row")),
            P(None, None, ("col", "row")),
            P(),
            P(),
        ),
        check_vma=False,
    )
```

profile of v0, /device:TPU:0, one launch (start us, length us, event | category | flops | bytes accessed | tf_op | source)
XLA Modules:
  0.0 390.2 jit_solution(12778961213633793991)
XLA Ops:
  27.2 9.6 %bitcast_add_fusion.2 = f32[3,96,1024]{1,0,2:T(4,128)} fusion(f32[3,3,1024]{1,0,2:T(4,128)} %copy.313, f32[3,96,1024]{1,0,2:T(4,128)S(1)} %copy.255, f32[3,1024]{0,1:T(8,128)S(1)} %copy.249), kind=kOutput, calls=%fused_computation.29 | convolution fusion | flops 10911744 | bytes 2408448 | tf_op jit(solution)/shard_map/xym,ykm->xkm/dot_general | solution.py:20
  38.9 12.2 %multiply_reduce_fusion.2 = (f32[48,1024]{0,1:T(8,128)}, f32[3,48,1024]{1,0,2:T(4,128)}) fusion(f32[3,1024]{0,1:T(8,128)S(1)} %copy.249, f32[3,3,1024]{1,0,2:T(4,128)} %copy.313, f32[3,48,1024]{1,0,2:T(4,128)} %copy.248), kind=kOutput, calls=%fused_computation.31 | convolution fusion | flops 5701632 | bytes 1425408 | tf_op jit(solution)/shard_map/xym,ykm->xkm/dot_general | solution.py:20
  54.6 7.0 %fusion.99 = f32[12,128,1024,1]{2,1,0,3:T(8,128)} fusion(f32[3,12,4,128]{3,2,1,0:T(4,128)S(1)} %bitcast.250, f32[3,12,4,1024]{3,2,1,0:T(4,128)S(1)} %reshape.204), kind=kOutput, calls=%fused_computation.137 | convolution fusion | flops 226492416 | bytes 6955008 | tf_op jit(solution)/shard_map/xhpi,xhpj->hij/dot_general | solution.py:99
  61.6 18.6 %fusion.88 = f32[12,128,1024]{2,0,1:T(8,128)} fusion(bf16[128,1024,128]{2,1,0:T(8,128)(2,1)} %param.15, bf16[128,12]{0,1:T(8,128)(2,1)S(1)} %copy-done.24), kind=kOutput, calls=%fused_computation.121 | convolution fusion | flops 402653184 | bytes 39848960 | tf_op jit(solution)/shard_map/ijc,ch->hij/dot_general | solution.py:105
  80.2 15.2 %fusion.98 = (f32[12,128]{1,0:T(8,128)S(1)}, f32[12,128,1024]{2,1,0:T(8,128)S(1)}) fusion(f32[12,128,1024,1]{2,1,0,3:T(8,128)} %fusion.99, f32[12,1024]{1,0:T(8,128)S(1)} %reduce_sum.118, f32[12,128]{1,0:T(8,128)S(1)} %reduce_sum.115, f32[12]{0:T(128)S(1)} %copy-done.26, f32[12,128,1024]{2,0,1:T(8,128)} %fusion.88, f32[12,16,128]{2,1,0:T(8,128)S(1)} %bitcast.257, ...), kind=kOutput, calls=%fused_computation.136 | convolution fusion | flops 317716992 | bytes 19821616 | tf_op jit(solution)/shard_map/hci,hcj->hij/dot_general | solution.py:98
  95.4 5.4 %all-gather.4 = f32[2,12,128]{2,1,0:T(8,128)} all-gather(f32[1,12,128]{2,1,0:T(8,128)S(1)} %bitcast.261), channel_id=2, replica_groups=mesh['row'=16,'col'=2] {'col'}, dimensions={0}, use_global_device_ids=true | all-gather | bytes 18432 | tf_op jit(solution)/shard_map/all_gather | solution.py:12
  100.8 14.1 %fusion.57 = f32[128,12,1024]{2,1,0:T(8,128)S(1)} fusion(bf16[128,1024,128]{2,1,0:T(8,128)(2,1)} %param.15, bf16[128,12,128]{2,0,1:T(8,128)(2,1)S(1)} %copy-done.4), kind=kOutput, calls=%fused_computation.57 | convolution fusion | flops 402653184 | bytes 40239104 | tf_op jit(solution)/shard_map/ijc,ihc->hij/dot_general | solution.py:111
  115.0 8.2 %fusion.100 = f32[12,128,1024]{2,1,0:T(8,128)} fusion(f32[12,16,128]{2,1,0:T(8,128)} %bitcast.262, f32[12,16,1024]{2,1,0:T(8,128)} %bitcast.255), kind=kOutput, calls=%fused_computation.138 | convolution fusion | flops 301989888 | bytes 7176192 | tf_op jit(solution)/shard_map/hci,hcj->hij/dot_general | solution.py:109
  123.2 14.2 %fusion.12 = (f32[12,128]{1,0:T(8,128)S(1)}, f32[12,128]{1,0:T(8,128)S(1)}, f32[12,128,1024]{2,1,0:T(8,128)}) fusion(f32[12,128,1024]{2,1,0:T(8,128)S(1)} %get-tuple-element.119, f32[12,128]{1,0:T(8,128)S(1)} %get-tuple-element.118, f32[128,12,1024]{2,1,0:T(8,128)S(1)} %fusion.57, f32[12,128,1024]{2,1,0:T(8,128)} %fusion.100, ...), kind=kOutput, calls=%fused_computation.22 | convolution fusion | flops 462418944 | bytes 26511360 | tf_op jit(solution)/shard_map/xhvi,xhvj->hij/dot_general | solution.py:110
  141.7 4.3 %all-gather.6 = f32[2,12,128]{2,1,0:T(8,128)S(1)} all-gather(f32[1,12,128]{2,1,0:T(8,128)S(1)} %bitcast.265), channel_id=4, replica_groups=mesh['row'=16,'col'=2] {'col'}, dimensions={0}, use_global_device_ids=true | all-gather | bytes 18432 | tf_op jit(solution)/shard_map/all_gather | solution.py:12
  146.2 8.8 %multiply_reduce_fusion = (f32[12]{0:T(128)S(1)}, f32[12,1024]{1,0:T(8,128)}, f32[12,128]{1,0:T(8,128)S(1)}, f32[12,128,1024]{2,1,0:T(8,128)S(1)}, bf16[12,128,1024]{2,1,0:T(8,128)(2,1)}) fusion(f32[12,128,1024,1]{2,1,0,3:T(8,128)S(1)} %bitcast.246, f32[12,1024]{1,0:T(8,128)} %copy-done.16, f32[12,128]{1,0:T(8,128)S(1)} %reduce_sum.115, ...), kind=kLoop, calls=%fused_computation.17 | loop fusion | flops 18860532 | bytes 28440624 | tf_op jit(solution)/shard_map/reduce_sum | solution.py:135
  157.7 5.4 %fusion.44 = f32[3,12,4,128]{3,2,0,1:T(4,128)S(1)} fusion(f32[12,128,1024]{2,1,0:T(8,128)S(1)} %get-tuple-element.102, f32[3,12,4,1024]{3,2,1,0:T(4,128)S(1)} %reshape.204, f32[3,12,4,128]{3,2,1,0:T(4,128)S(1)} %bitcast.251, f32[12,128]{1,0:T(8,128)S(1)} %get-tuple-element.97, f32[12]{0:T(128)S(1)} %copy-done.28), kind=kOutput, calls=%fused_computation.52 | convolution fusion | flops 226547712 | bytes 7034928 | tf_op jit(solution)/shard_map/hij,xhpj->xhpi/dot_general | solution.py:147
  165.7 6.1 %fusion.19 = f32[3,12,8,1024]{3,2,0,1:T(8,128)S(1)} fusion(f32[12,128,1024]{2,1,0:T(8,128)} %copy-done.3, f32[12,128]{1,0:T(8,128)S(1)} %get-tuple-element.103, f32[12,128]{1,0:T(8,128)S(1)} %get-tuple-element.106, f32[3,96,128]{2,1,0:T(8,128)S(1)} %copy-done.12), kind=kOutput, calls=%fused_computation.32 | convolution fusion | flops 456130560 | bytes 7630848 | tf_op jit(solution)/shard_map/hij,xhvi->xhvj/dot_general | solution.py:189
  175.9 5.2 %fusion.28 = f32[3,12,4,1024]{3,2,0,1:T(4,128)S(1)} fusion(f32[12,128,1024]{2,1,0:T(8,128)} %copy-done.2, f32[3,12,4,1024]{3,2,1,0:T(4,128)S(1)} %reshape.204, f32[12,1024]{1,0:T(8,128)S(1)} %copy-done.19, f32[12]{0:T(128)S(1)} %copy-done.27, f32[3,12,4,128]{3,2,1,0:T(4,128)S(1)} %bitcast.252), kind=kOutput, calls=%fused_computation.36 | convolution fusion | flops 226934784 | bytes 7594032 | tf_op jit(solution)/shard_map/hij,xhpi->xhpj/dot_general | solution.py:185
  188.5 7.9 %convolution_multiply_fusion.1 = f32[12,128,16]{1,2,0:T(8,128)S(1)} fusion(f32[12,128,1024]{2,1,0:T(8,128)} %copy-done.2, f32[12,16,1024]{2,1,0:T(8,128)S(1)} %bitcast.244), kind=kOutput, calls=%fused_computation.49 | convolution fusion | flops 302014464 | bytes 7176192 | tf_op jit(solution)/shard_map/hij,hcj->hci/dot_general | solution.py:139
  197.2 5.5 %convolution_multiply_fusion = f32[12,1024,16]{1,2,0:T(8,128)S(1)} fusion(f32[12,128,1024]{2,1,0:T(8,128)} %copy-done.2, f32[12,16,128]{2,1,0:T(8,128)S(1)} %bitcast.258), kind=kOutput, calls=%fused_computation.33 | convolution fusion | flops 302186496 | bytes 7176192 | tf_op jit(solution)/shard_map/hij,hci->hcj/dot_general | solution.py:177
  204.1 6.5 %fusion.94 = f32[12,1024,16]{1,2,0:T(8,128)S(1)} fusion(f32[12,16,128]{2,1,0:T(8,128)S(1)} %bitcast.263, f32[12,128,1024]{2,1,0:T(8,128)} %copy-done.3, f32[12,128]{1,0:T(8,128)S(1)} %get-tuple-element.103, f32[12,128]{1,0:T(8,128)S(1)} %copy-done.23), kind=kOutput, calls=%fused_computation.133 | convolution fusion | flops 305135616 | bytes 7188480 | tf_op jit(solution)/shard_map/hij,hci->hcj/dot_general | solution.py:179
  212.1 7.8 %fusion.33 = f32[3,12,8,128]{3,2,0,1:T(8,128)S(1)} fusion(f32[12,128,1024]{2,1,0:T(8,128)} %copy-done.3, f32[12,128]{1,0:T(8,128)S(1)} %get-tuple-element.118, f32[3,96,1024]{2,1,0:T(8,128)S(1)} %copy.257), kind=kOutput, calls=%fused_computation.41 | convolution fusion | flops 454557696 | bytes 7624704 | tf_op jit(solution)/shard_map/hij,xhvj->xhvi/dot_general | solution.py:117
  223.2 14.1 %fusion.53 = f32[128,12]{0,1:T(8,128)S(1)} fusion(bf16[128,1024,128]{2,1,0:T(8,128)(2,1)} %param.15, bf16[12,128,1024]{2,1,0:T(8,128)(2,1)S(1)} %convert_element_type.9), kind=kOutput, calls=%fused_computation.55 | convolution fusion | flops 402654720 | bytes 36706304 | tf_op jit(solution)/shard_map/ijc,hij->ch/dot_general | solution.py:132
  237.3 23.9 %fusion.15 = f32[128,1024,128]{2,1,0:T(8,128)} fusion(bf16[12,128,1024]{2,1,0:T(8,128)(2,1)S(1)} %convert_element_type.9, bf16[128,12]{0,1:T(8,128)(2,1)S(1)} %copy-done.24), kind=kOutput, calls=%fused_computation.25 | convolution fusion | flops 402653184 | bytes 70257664 | tf_op jit(solution)/shard_map/hij,ch->ijc/dot_general | solution.py:129
  263.4 6.1 %all-gather.3 = f32[6,12,8,128]{3,2,0,1:T(8,128)S(1)} all-gather(f32[3,12,8,128]{3,2,0,1:T(8,128)S(1)} %fusion.33), channel_id=5, replica_groups=mesh['row'=16,'col'=2] {'col'}, dimensions={0}, use_global_device_ids=true | all-gather | bytes 442368 | tf_op jit(solution)/shard_map/all_gather | solution.py:12
  270.7 41.3 %all-reduce.1 = (f32[128,12]{0,1:T(8,128)}, f32[12]{0:T(128)S(1)}) all-reduce(f32[128,12]{0,1:T(8,128)S(1)} %fusion.53, f32[12]{0:T(128)S(1)} %get-tuple-element.95), channel_id=1, replica_groups=mesh['row'=16,'col'=2] {'row','col'}, use_global_device_ids=true, to_apply=%region_19.20 | all-reduce | flops 1548 | bytes 12384 | tf_op jit(solution)/shard_map/psum | solution.py:208
  313.8 36.3 %add_convert_fusion = bf16[128,1024,128]{2,1,0:T(8,128)(2,1)} fusion(f32[128,1024,128]{2,1,0:T(8,128)} %fusion.15, bf16[12,128,1024]{2,1,0:T(8,128)(2,1)} %get-tuple-element.107, bf16[128,12,128]{2,0,1:T(8,128)(2,1)S(1)} %copy-done.4), kind=kOutput, calls=%fused_computation | convolution fusion | flops 452984832 | bytes 104202240 | tf_op jit(solution)/shard_map/hij,ihc->ijc/dot_general | solution.py:130
  363.4 19.5 %reduce-scatter.14.cloned.1.call-done = f32[192,64]{0,1:T(8,128)} async-done(((f32[192,1024]{0,1:T(8,128)}), f32[192,64]{0,1:T(8,128)}) %reduce-scatter.14.cloned.1.call-update) | async-done | bytes 49168 | tf_op jit(solution)/shard_map/reduce_scatter | solution.py:196
  (172 shorter events, 69.6 us)
Async XLA Ops:
  8.0 72.2 %copy-start = (f32[192,1024]{1,0:T(8,128)S(1)}, f32[192,1024]{1,0:T(8,128)}, u32[]{:S(2)}) copy-start(f32[192,1024]{1,0:T(8,128)} %param.19) | copy-start | bytes 2359300
  8.0 342.0 %reduce-scatter.16.cloned.1.call-start = ((), (), s32[]{:S(2)}) async-start(), calls=%async_computation.8 | async-start | bytes 196608
  38.9 15.7 %copy-start.6 = (f32[3,48,128]{2,1,0:T(8,128)S(1)}, f32[3,48,128]{2,1,0:T(8,128)}, u32[]{:S(2)}) copy-start(f32[3,48,128]{2,1,0:T(8,128)} %copy.251) | copy-start | bytes 221188
  52.6 27.6 %copy-start.16 = (f32[12,1024]{1,0:T(8,128)}, f32[12,1024]{1,0:T(8,128)S(1)}, u32[]{:S(2)}) copy-start(f32[12,1024]{1,0:T(8,128)S(1)} %reduce_sum.118) | copy-start | bytes 147460
  61.6 18.6 %copy-start.17 = (f32[192,128]{1,0:T(8,128)S(1)}, f32[192,128]{1,0:T(8,128)}, u32[]{:S(2)}) copy-start(f32[192,128]{1,0:T(8,128)} %param.18) | copy-start | bytes 294916
  61.6 18.6 %copy-start.25 = (pred[1024]{0:T(1024)(128)(4,1)S(1)}, pred[1024]{0:T(1024)(128)(4,1)}, u32[]{:S(2)}) copy-start(pred[1024]{0:T(1024)(128)(4,1)} %add_compare_fusion) | copy-start | bytes 3076
  61.6 18.6 %copy-start.26 = (f32[12]{0:T(128)S(1)}, f32[12]{0:T(128)}, u32[]{:S(2)}) copy-start(f32[12]{0:T(128)} %get-tuple-element.113) | copy-start | bytes 148
  80.2 20.6 %copy-start.4 = (bf16[128,12,128]{2,0,1:T(8,128)(2,1)S(1)}, bf16[128,12,128]{2,0,1:T(8,128)(2,1)}, u32[]{:S(2)}) copy-start(bf16[128,12,128]{2,0,1:T(8,128)(2,1)} %param.29) | copy-start | bytes 1179652
  95.4 50.7 %copy-start.3 = (f32[12,128,1024]{2,1,0:T(8,128)}, f32[12,128,1024]{2,1,0:T(8,128)S(1)}, u32[]{:S(2)}) copy-start(f32[12,128,1024]{2,1,0:T(8,128)S(1)} %get-tuple-element.119) | copy-start | bytes 18874372
  115.0 31.2 %slice-start = ((s8[6291456]{0:T(1024)(128)(4,1)}), s8[4194304]{0:T(1024)(128)(4,1)S(1)}, s32[]{:S(2)}) async-start(s8[6291456]{0:T(1024)(128)(4,1)} %bitcast.245), calls=%async_computation.11 | async-start | bytes 8388608
  123.2 22.9 %copy-start.21 = (f32[2,12,128]{2,1,0:T(8,128)S(1)}, f32[2,12,128]{2,1,0:T(8,128)}, u32[]{:S(2)}) copy-start(f32[2,12,128]{2,1,0:T(8,128)} %all-gather.4) | copy-start | bytes 36868
  123.2 22.9 %slice-start.1 = ((s8[6291456]{0:T(1024)(128)(4,1)}), s8[2097152]{0:T(1024)(128)(4,1)S(1)}, s32[]{:S(2)}) async-start(s8[6291456]{0:T(1024)(128)(4,1)} %bitcast.245), calls=%async_computation.12 | async-start | bytes 4194304
  146.1 19.6 %copy-start.22 = (f32[12,128]{1,0:T(8,128)}, f32[12,128]{1,0:T(8,128)S(1)}, u32[]{:S(2)}) copy-start(f32[12,128]{1,0:T(8,128)S(1)} %get-tuple-element.106) | copy-start | bytes 18436
  165.7 188.2 %all-reduce.4.cloned.1.call-start = ((), (), s32[]{:S(2)}) async-start(), calls=%async_computation.10 | async-start | bytes 4194304
  175.8 182.9 %reduce-scatter.18.cloned.1.call-start = ((), (), s32[]{:S(2)}) async-start(), calls=%async_computation.9 | async-start | bytes 1114112
  188.4 175.0 %reduce-scatter.10.cloned.1.call-start = ((), (), s32[]{:S(2)}) async-start(), calls=%async_computation.5 | async-start | bytes 196608 | tf_op jit(solution)/shard_map/reduce_scatter | solution.py:151
  197.2 166.3 %reduce-scatter.12.cloned.1.call-start = ((), (), s32[]{:S(2)}) async-start(), calls=%async_computation.6 | async-start | bytes 1114112 | tf_op jit(solution)/shard_map/reduce_scatter | solution.py:195
  204.0 178.9 %reduce-scatter.14.cloned.1.call-start = ((), (), s32[]{:S(2)}) async-start(), calls=%async_computation.7 | async-start | bytes 1114112 | tf_op jit(solution)/shard_map/reduce_scatter | solution.py:196
  237.3 25.8 %copy-start.9 = (f32[128,3,96]{2,1,0:T(4,128)S(1)}, f32[128,3,96]{2,1,0:T(4,128)}, u32[]{:S(2)}) copy-start(f32[128,3,96]{2,1,0:T(4,128)} %copy-done.8) | copy-start | bytes 442372
  237.3 32.7 %copy-start.11 = (f32[3,96,128]{1,0,2:T(4,128)S(1)}, f32[3,96,128]{1,0,2:T(4,128)}, u32[]{:S(2)}) copy-start(f32[3,96,128]{1,0,2:T(4,128)} %copy-done.10) | copy-start | bytes 442372
  237.3 74.7 %copy-start.29 = (f32[12]{0:T(128)S(1)}, f32[12]{0:T(128)}, u32[]{:S(2)}) copy-start(f32[12]{0:T(128)} %param.17) | copy-start | bytes 148
  237.3 75.2 %copy-start.30 = (u32[32]{0:T(128)S(1)}, u32[32]{0:T(128)}, u32[]{:S(2)}) copy-start(u32[32]{0:T(128)} %constant.61) | copy-start | bytes 388
  313.7 37.3 %copy-start.14 = (f32[3,48,128]{1,0,2:T(4,128)S(1)}, f32[3,48,128]{1,0,2:T(4,128)}, u32[]{:S(2)}) copy-start(f32[3,48,128]{1,0,2:T(4,128)} %copy-done.13) | copy-start | bytes 221188
  313.8 69.2 %copy-start.1 = (f32[192,1024]{1,0:T(8,128)S(1)}, f32[192,1024]{1,0:T(8,128)}, u32[]{:S(2)}) copy-start(f32[192,1024]{1,0:T(8,128)} %param.19) | copy-start | bytes 2359300
  (15 other events, 109.4 us)
Sparse Core Ops, SparseCore 0:
  165.8 12.1 reduce-scatter.15
  188.6 59.5 reduce-scatter.17
  251.0 9.4 reduce-scatter.9
  264.5 57.6 reduce-scatter.11
  326.2 56.6 reduce-scatter.13
Sparse Core Ops, SparseCore 1:
  175.9 100.9 all-reduce.3
where the time goes:
time: 397 us; the launch traced here: 390 us
  matrix products  227 us (57%)
  blocking collectives  61.4 us (15%)
  local copies, waits for them, and re-layouts  47.1 us (12%)
  waiting for transfers between devices  19.6 us (5%)
  other arithmetic  17.9 us (5%)
  between operations  17.5 us (4%)
    psum x1, blocking collectives, per_device(): lax.psum((weight_part, distance_part), ('row', 'col'))  41.3 us
    dot_general x1, matrix products, per_device(): jnp.einsum('hij,ihc->ijc', attn_rounded, grad_pair, preferred_element_typ...  36.3 us
    unnamed x87, local copies, waits for them, and re-layouts  25.1 us
    dot_general x1, matrix products, per_device(): jnp.einsum('hij,ch->ijc', grad_rounded, bias_weight, preferred_element_ty...  23.9 us
    dot_general x3, matrix products, globalize(): jnp.einsum('xym,ykm->xkm', rotation, local, precision=HIGHEST)  22.9 us
    all_gather x4, blocking collectives, joined(): pieces = jax.tree.map(lambda part: lax.all_gather(part, axis), value)  20.2 us
    reduce_scatter x1, waiting for transfers between devices, per_device(): lax.psum_scatter(value_flat, 'row', scatter_dimension=1, tiled=True)  19.5 us
    dot_general x1, matrix products, per_device(): jnp.einsum('ijc,ch->hij', pair_rep, bias_weight, preferred_element_type=j...  18.6 us
  transfers between devices with their start and end apart: 6, of which 1 were waited for; matrix products, arithmetic and copies ran while one was open for 38% of the time, Pallas kernels for 0%

commit v1 on v0

v1 whole, which is shorter than its diff:
```python
import functools
import math

import jax
import jax.numpy as jnp
from jax import lax
from jax.experimental import pallas as pl
from jax.experimental.pallas import tpu as pltpu
from jax.sharding import PartitionSpec as P

F32 = jnp.float32
BF16 = jnp.bfloat16
PAD = 16
VMEM_LIMIT = 60 * 1024 * 1024


def dot(a, b, dims):
    return lax.dot_general(a, b, (dims, ((), ())), preferred_element_type=F32)


TN = ((0,), (0,))
NT = ((1,), (1,))
NN = ((1,), (0,))


def split2(x):
    hi = x.astype(BF16)
    return hi, (x - hi.astype(F32)).astype(BF16)


def split3(x):
    hi = x.astype(BF16)
    rest = x - hi.astype(F32)
    mid = rest.astype(BF16)
    return hi, mid, (rest - mid.astype(F32)).astype(BF16)


def forward_kernel(
    heads, block, scale, limit_ref, pair, bias_w, gpair, qcat, kcat, gcat, vcat,
    e_out, d_out, stat_out, lbase, dbase, rows_buf,
):
    step = pl.program_id(0)

    @pl.when(step == 0)
    def _():
        def head(h, carry):
            q0, q1, q2 = split3(qcat[h])
            k0, k1, k2 = split3(kcat[h])
            lbase[h] = dot(
                jnp.concatenate([q0, q0, q1, q0, q2, q1], 0),
                jnp.concatenate([k0, k1, k0, k2, k0, k1], 0),
                TN,
            )
            g0, g1 = split2(gcat[h])
            v0, v1 = split2(vcat[h])
            dbase[h] = dot(
                jnp.concatenate([g0, g0, g1], 0), jnp.concatenate([v0, v1, v0], 0), TN
            )
            return carry

        lax.fori_loop(0, heads, head, 0)

    for r in range(block):
        w = jnp.concatenate([bias_w[...], gpair[r]], 0)
        rows_buf[r] = dot(w, pair[r], NT)
    cols = pair.shape[1]
    rows = pl.ds(pl.multiple_of(step * block, block), block)
    valid = lax.broadcasted_iota(jnp.int32, (block, cols), 1) < limit_ref[0]
    lane = lax.broadcasted_iota(jnp.int32, (block, 128), 1)
    peaks = jnp.zeros((block, 128), F32)
    totals = jnp.ones((block, 128), F32)
    uppers = jnp.zeros((block, 128), F32)
    for h in range(heads):
        logit = lbase[h, rows, :] + scale * rows_buf[:, h, :]
        logit = jnp.where(valid, logit, F32(-1000000000.0))
        peak = jnp.max(logit, axis=1, keepdims=True)
        e = jnp.exp(logit - peak)
        d = dbase[h, rows, :] + rows_buf[:, PAD + h, :]
        e_out[h] = e
        d_out[h] = d
        peaks = jnp.where(lane == h, peak, peaks)
        totals = jnp.where(lane == h, jnp.sum(e, axis=1, keepdims=True), totals)
        uppers = jnp.where(lane == h, jnp.sum(e * d, axis=1, keepdims=True), uppers)
    stat_out[0] = peaks
    stat_out[1] = totals
    stat_out[2] = uppers


def backward_kernel(
    heads, block, nq, nv, vwidth, pair, e_in, d_in, stats, own, w_hi, w_lo, gpair, qcat, kcat,
    gcat, vcat, pg_out, key_out, query_out, w_out, rows_buf, att_all, dl_all,
):
    step = pl.program_id(0)
    rows = pl.ds(pl.multiple_of(step * block, block), block)

    @pl.when(step == 0)
    def _():
        rows_buf[...] = jnp.zeros_like(rows_buf)
        w_out[...] = jnp.zeros_like(w_out)

    peers = stats.shape[0]
    top = stats[0, 0]
    for c in range(1, peers):
        top = jnp.maximum(top, stats[c, 0])
    total = jnp.zeros_like(top)
    upper = jnp.zeros_like(top)
    for c in range(peers):
        f = jnp.exp(stats[c, 0] - top)
        total = total + stats[c, 1] * f
        upper = upper + stats[c, 2] * f
    factor = jnp.exp(own[0] - top) / total
    delta = upper / total
    for h in range(heads):
        att = e_in[h] * factor[:, h : h + 1]
        dl = att * (d_in[h] - delta[:, h : h + 1])
        att_all[h, rows, :] = att
        dl_all[h, rows, :] = dl
        rows_buf[:, h, :] = dl
        rows_buf[:, PAD + h, :] = att
    acc = w_out[...]
    for r in range(block):
        a = rows_buf[r].astype(BF16)
        lhs = jnp.concatenate([a, a[:PAD]], 0)
        rhs = jnp.concatenate([w_hi[...], gpair[r], w_lo[...]], 0)
        pg_out[r] = dot(lhs, rhs, TN).astype(BF16)
        acc = acc + dot(a[:PAD], pair[r], NN)
    w_out[...] = acc

    @pl.when(step == pl.num_programs(0) - 1)
    def _():
        def head(h, carry):
            d0, d1 = split2(dl_all[h])
            a0, a1 = split2(att_all[h])
            q = jnp.concatenate(split2(qcat[h]), 0)
            k = jnp.concatenate(split2(kcat[h]), 0)
            g = jnp.concatenate(split2(gcat[h]), 0)
            v = jnp.concatenate(split2(vcat[h]), 0)
            kk = dot(q, d0, NN) + dot(q, d1, NN)
            key_out[h, :nq, :] = kk[:nq] + kk[nq:]
            vv = dot(g, a0, NN) + dot(g, a1, NN)
            half = g.shape[0] // 2
            key_out[h, nq:, :] = vv[:nv] + vv[half : half + nv]
            qq = dot(k, d0, NT) + dot(k, d1, NT)
            query_out[h, :nq, :] = qq[:nq] + qq[nq:]
            oo = dot(v, a0, NT) + dot(v, a1, NT)
            query_out[h, nq:, :] = oo[vwidth:nv] + oo[half + vwidth : half + nv]
            return carry

        lax.fori_loop(0, heads, head, 0)


def turn(rotation, local):
    return jnp.sum(rotation[:, :, None, :] * local[None], axis=1)


def turn_back(rotation, vector):
    return jnp.sum(rotation[:, :, None, :] * vector[:, None], axis=0)


def frame_terms(grad_global, local):
    rotation_part = jnp.sum(grad_global[:, None] * local[None], axis=2)
    return jnp.concatenate([rotation_part, jnp.sum(grad_global, axis=1)[:, None, :]], axis=1)


def by_head(x, heads):
    points = x.shape[1] // heads
    return x.reshape(3, heads, points, -1).transpose(1, 0, 2, 3).reshape(heads, 3 * points, -1)


def by_axis(x):
    heads, rows, m = x.shape
    return x.reshape(heads, 3, rows // 3, m).transpose(1, 0, 2, 3).reshape(3, heads * rows // 3, m)


def pad_rows(x, rows):
    return jnp.pad(x, ((0, 0), (0, rows - x.shape[1]), (0, 0)))


def per_device(
    pair_rep, bias_weight, head_weight, queries, key_vectors, values, query_points, key_points,
    value_points, rotations, translations, residue_count, grad_output, grad_points, grad_pair,
):
    channels, heads = bias_weight.shape
    width = queries.shape[0] // heads
    qpoints = query_points.shape[1] // heads
    vpoints = value_points.shape[1] // heads
    n_rows = queries.shape[1]
    n_cols = key_vectors.shape[1]
    logit_scale = math.sqrt(1.0 / 3.0)
    point_scale = math.sqrt(2.0 / (9.0 * qpoints))
    inner_scale = 1.0 / math.sqrt(width)
    coef = 0.5 * logit_scale * point_scale * jax.nn.softplus(head_weight)
    row_start = lax.axis_index("row") * n_rows
    col_start = lax.axis_index("col") * n_cols
    rot_rows = lax.dynamic_slice_in_dim(rotations, row_start, n_rows, 2)
    shift_rows = lax.dynamic_slice_in_dim(translations, row_start, n_rows, 1)
    rot_cols = lax.dynamic_slice_in_dim(rotations, col_start, n_cols, 2)
    shift_cols = lax.dynamic_slice_in_dim(translations, col_start, n_cols, 1)
    qg = by_head(turn(rot_rows, query_points) + shift_rows[:, None, :], heads)
    kg = by_head(turn(rot_cols, key_points) + shift_cols[:, None, :], heads)
    vg = by_head(turn(rot_cols, value_points) + shift_cols[:, None, :], heads)
    grad_flat = turn(rot_rows, grad_points)
    gg = by_head(grad_flat, heads)
    q = queries.reshape(heads, width, n_rows)
    k = key_vectors.reshape(heads, width, n_cols)
    qsize = width + 3 * qpoints
    nq = -(-(qsize + 2) // 16) * 16
    nv = width + 3 * vpoints
    nvp = -(-nv // 16) * 16
    c3 = coef[:, None, None]
    q_square = jnp.sum(qg * qg, axis=1, keepdims=True)
    k_square = jnp.sum(kg * kg, axis=1, keepdims=True)
    qcat = pad_rows(
        jnp.concatenate(
            [
                logit_scale * inner_scale * q,
                2.0 * c3 * qg,
                jnp.broadcast_to(-c3, (heads, 1, n_rows)),
                -c3 * q_square,
            ],
            axis=1,
        ),
        nq,
    )
    kcat = pad_rows(
        jnp.concatenate([k, kg, k_square, jnp.ones((heads, 1, n_cols), F32)], axis=1), nq
    )
    gcat = pad_rows(
        jnp.concatenate([grad_output.reshape(heads, width, n_rows), gg], axis=1), nvp
    )
    vcat = pad_rows(jnp.concatenate([values.reshape(heads, width, n_cols), vg], axis=1), nvp)
    w_t = jnp.pad(bias_weight.T, ((0, PAD - heads), (0, 0)))
    scaled = logit_scale * w_t.astype(F32)
    w_hi, w_lo = split2(scaled)
    gpair = pad_rows(grad_pair, PAD)
    limit = residue_count - col_start

    block = 8
    grid = (n_rows // block,)
    whole = lambda *shape: pl.BlockSpec(shape, lambda i: (0,) * len(shape))
    pair_spec = pl.BlockSpec((block, n_cols, channels), lambda i: (i, 0, 0))
    gpair_spec = pl.BlockSpec((block, PAD, channels), lambda i: (i, 0, 0))
    hij_spec = pl.BlockSpec((heads, block, n_cols), lambda i: (0, i, 0))
    stat_spec = pl.BlockSpec((3, block, 128), lambda i: (0, i, 0))
    cat_specs = [
        whole(heads, nq, n_rows),
        whole(heads, nq, n_cols),
        whole(heads, nvp, n_rows),
        whole(heads, nvp, n_cols),
    ]
    params = pltpu.CompilerParams(
        dimension_semantics=("arbitrary",), vmem_limit_bytes=VMEM_LIMIT
    )
    hij = jax.ShapeDtypeStruct((heads, n_rows, n_cols), F32)
    e_all, d_all, own = pl.pallas_call(
        functools.partial(forward_kernel, heads, block, logit_scale),
        grid=grid,
        in_specs=[
            pl.BlockSpec(memory_space=pltpu.SMEM),
            pair_spec,
            whole(PAD, channels),
            gpair_spec,
            *cat_specs,
        ],
        out_specs=[hij_spec, hij_spec, stat_spec],
        out_shape=[hij, hij, jax.ShapeDtypeStruct((3, n_rows, 128), F32)],
        scratch_shapes=[
            pltpu.VMEM((heads, n_rows, n_cols), F32),
            pltpu.VMEM((heads, n_rows, n_cols), F32),
            pltpu.VMEM((block, 2 * PAD, n_cols), F32),
        ],
        compiler_params=params,
    )(limit, pair_rep, w_t, gpair, qcat, kcat, gcat, vcat)

    stats = lax.all_gather(own, "col")
    peers = stats.shape[0]
    nk = nq + nv
    nr = nq + nv - width
    pair_grad, key_out, query_out, w_out = pl.pallas_call(
        functools.partial(backward_kernel, heads, block, nq, nv, width),
        grid=grid,
        in_specs=[
            pair_spec,
            hij_spec,
            hij_spec,
            pl.BlockSpec((peers, 3, block, 128), lambda i: (0, 0, i, 0)),
            stat_spec,
            whole(PAD, channels),
            whole(PAD, channels),
            gpair_spec,
            *cat_specs,
        ],
        out_specs=[
            pair_spec,
            whole(heads, nk, n_cols),
            whole(heads, nr, n_rows),
            whole(PAD, channels),
        ],
        out_shape=[
            jax.ShapeDtypeStruct(pair_rep.shape, BF16),
            jax.ShapeDtypeStruct((heads, nk, n_cols), F32),
            jax.ShapeDtypeStruct((heads, nr, n_rows), F32),
            jax.ShapeDtypeStruct((PAD, channels), F32),
        ],
        scratch_shapes=[
            pltpu.VMEM((block, 2 * PAD, n_cols), F32),
            pltpu.VMEM((heads, n_rows, n_cols), F32),
            pltpu.VMEM((heads, n_rows, n_cols), F32),
        ],
        compiler_params=params,
    )(pair_rep, e_all, d_all, stats, own, w_hi, w_lo, gpair, qcat, kcat, gcat, vcat)

    distance_part = jnp.sum(
        q_square[:, 0] * query_out[:, qsize + 1] + query_out[:, qsize], axis=1
    ) - 2.0 * jnp.sum(qg * query_out[:, width:qsize], axis=(1, 2))
    weight_part = logit_scale * w_out[:heads].T
    small = jnp.concatenate([weight_part.reshape(-1), distance_part])

    key_sum = lax.psum_scatter(
        key_out.reshape(heads * nk, n_cols), "row", scatter_dimension=1, tiled=True
    ).reshape(heads, nk, -1)
    query_sum = lax.psum_scatter(
        query_out.reshape(heads * nr, n_rows), "col", scatter_dimension=1, tiled=True
    ).reshape(heads, nr, -1)
    small = lax.psum(small, ("row", "col"))
    weight_total = small[: channels * heads].reshape(channels, heads)
    head_weight_grad = (
        small[channels * heads :]
        * (-0.5 * logit_scale * point_scale)
        * jax.nn.sigmoid(head_weight)
    )

    share = query_sum.shape[2]
    start = lax.axis_index("col") * share
    own_rows = lambda x: lax.dynamic_slice_in_dim(x, start, share, x.ndim - 1)
    rot_own = own_rows(rot_rows)
    shift_own = own_rows(shift_rows)
    query_grad = (logit_scale * inner_scale * query_sum[:, :width]).reshape(heads * width, share)
    dqg = by_axis(
        -2.0 * c3 * (own_rows(qg) * query_sum[:, qsize + 1][:, None] - query_sum[:, width:qsize])
    )
    point_out = by_axis(query_sum[:, nq:])
    query_point_grad = turn_back(rot_own, dqg)
    cotan_own = own_rows(grad_points)
    out_part = jnp.sum((point_out - shift_own[:, None, :])[:, None] * cotan_own[None], axis=2)
    out_part = jnp.concatenate(
        [out_part, -jnp.sum(own_rows(grad_flat), axis=1)[:, None, :]], axis=1
    )
    query_frame_grad = frame_terms(dqg, own_rows(query_points)) + out_part

    kshare = key_sum.shape[2]
    kstart = lax.axis_index("row") * kshare
    own_cols = lambda x: lax.dynamic_slice_in_dim(x, kstart, kshare, x.ndim - 1)
    rot_keys = own_cols(rot_cols)
    key_grad = key_sum[:, :width].reshape(heads * width, kshare)
    value_grad = key_sum[:, nq : nq + width].reshape(heads * width, kshare)
    dkg = by_axis(
        key_sum[:, width:qsize] + 2.0 * own_cols(kg) * key_sum[:, qsize][:, None]
    )
    dvg = by_axis(key_sum[:, nq + width :])
    key_point_grad = turn_back(rot_keys, dkg)
    value_point_grad = turn_back(rot_keys, dvg)
    key_frame_grad = frame_terms(dkg, own_cols(key_points)) + frame_terms(
        dvg, own_cols(value_points)
    )
    return (
        pair_grad, query_grad, query_point_grad, query_frame_grad, key_grad, value_grad,
        key_point_grad, value_point_grad, key_frame_grad, weight_total, head_weight_grad,
    )


def solution(mesh):
    return jax.shard_map(
        per_device,
        mesh=mesh,
        in_specs=(
            P("row", "col", None),
            P(),
            P(),
            P(None, "row"),
            P(None, "col"),
            P(None, "col"),
            P(None, None, "row"),
            P(None, None, "col"),
            P(None, None, "col"),
            P(),
            P(),
            P(),
            P(None, "row"),
            P(None, None, "row"),
            P("row", None, None),
        ),
        out_specs=(
            P("row", "col", None),
            P(None, ("row", "col")),
            P(None, None, ("row", "col")),
            P(None, None, ("row", "col")),
            P(None, ("col", "row")),
            P(None, ("col", "row")),
            P(None, None, ("col", "row")),
            P(None, None, ("col", "row")),
            P(None, None, ("col", "row")),
            P(),
            P(),
        ),
        check_vma=False,
    )
```

time: 397 us -> 214 us (0.54); the launches traced: 390 us -> 213 us
  matrix products: 227 us -> 0 us
  Pallas kernels: 0 us -> 79.1 us
  local copies, waits for them, and re-layouts: 47.1 us -> 22.7 us
  waiting for transfers between devices: 19.6 us -> 34 us
  blocking collectives: 61.4 us -> 50.8 us
  other arithmetic: 17.9 us -> 10.5 us
    dot_general x27 -> x0, matrix products: 227 us -> none  [the longest x1 36.3 us: per_device(): jnp.einsum('hij,ihc->ijc', attn_rounded, grad_pair, preferred_element_typ...]
    pallas_call x0 -> x2, Pallas kernels: none -> 79.1 us  [the longest x1 48 us: per_device(): pl.pallas_call(functools.partial(backward_kernel, heads, block, nq, nv, w...]
    unnamed x9 -> x4, waiting for transfers between devices: 0.1 us -> 34 us
    reduce_scatter x3 -> x0, waiting for transfers between devices: 19.5 us -> none  [the longest x1 19.5 us: per_device(): lax.psum_scatter(value_flat, 'row', scatter_dimension=1, tiled=True)]
    unnamed x87 -> x37, local copies, waits for them, and re-layouts: 25.1 us -> 14.8 us
    all_gather x4 -> x1, blocking collectives: 20.2 us -> 11.1 us  [per_device(): stats = lax.all_gather(own, 'col')]
    reshape x6 -> x9, local copies, waits for them, and re-layouts: 7.48 us -> 0.52 us  [the longest x3 0.24 us: by_head(): x.reshape(3, heads, points, -1).transpose(1, 0, 2, 3)]
    reduce_sum x4 -> x12, other arithmetic: 9.09 us -> 4.03 us  [the longest x4 1.57 us: turn(): return jnp.sum(rotation[:, :, None, :] * local[None], axis=1)]
  transfers between devices with their start and end apart: 6 -> 2, of which waited for: 1 -> 1; matrix products, arithmetic and copies ran while one was open for 38% -> 5% of each run, Pallas kernels for 0% -> 0%
where the time goes in v1:
time: 214 us; the launch traced here: 213 us
  Pallas kernels  79.1 us (37%)
  blocking collectives  50.8 us (24%)
  waiting for transfers between devices  34 us (16%)
  local copies, waits for them, and re-layouts  22.7 us (11%)
  between operations  15.3 us (7%)
  other arithmetic  10.5 us (5%)
    pallas_call x1, Pallas kernels, per_device(): pl.pallas_call(functools.partial(backward_kernel, heads, block, nq, nv, w...  48 us
    psum x1, blocking collectives, per_device(): small = lax.psum(small, ('row', 'col'))  39.7 us
    unnamed x4, waiting for transfers between devices  34 us
    pallas_call x1, Pallas kernels, per_device(): pl.pallas_call(functools.partial(forward_kernel, heads, block, logit_scal...  31.1 us
    unnamed x37, local copies, waits for them, and re-layouts  14.8 us
    all_gather x1, blocking collectives, per_device(): stats = lax.all_gather(own, 'col')  11.1 us
  transfers between devices with their start and end apart: 2, of which 1 were waited for; matrix products, arithmetic and copies ran while one was open for 5% of the time, Pallas kernels for 0%

profile of v1, /device:TPU:0, one launch (start us, length us, event | category | flops | bytes accessed | tf_op | source)
XLA Modules:
  0.0 212.6 jit_solution(5669728141161759935)
XLA Ops:
  7.2 0.8 constant_dynamic-slice_fusion.8
  8.8 1.3 multiply_reduce_fusion.1
  15.4 0.9 pad.25.gpair
  16.6 1.3 pad.27.kcat
  18.1 1.7 select_maximum_fusion.vcat
  19.8 0.7 select_maximum_fusion.1.gcat
  20.6 0.7 select_maximum_fusion.2.qcat
  21.3 31.1 %shard_map.230 = (f32[12,128,1024]{2,1,0:T(8,128)}, f32[12,128,1024]{2,1,0:T(8,128)}, f32[3,128,128]{2,1,0:T(8,128)}) custom-call(s32[1]{0:T(128)S(6)} %sub.28.limit_ref, bf16[128,1024,128]{2,1,0:T(8,128)(2,1)} %pair.3, bf16[16,128]{1,0:T(8,128)(2,1)} %pad.24.bias_w, bf16[128,16,128]{2,1,0:T(8,128)(2,1)} %pad.25.gpair, ...), custom_call_target="tpu_custom_call" | custom-call | tf_op jit(solution)/shard_map/pallas_call | solution.py:255
  52.4 11.1 %all-gather = f32[6,128,128]{2,1,0:T(8,128)} all-gather(f32[3,128,128]{2,1,0:T(8,128)} %get-tuple-element.20.own), channel_id=2, replica_groups=mesh['row'=16,'col'=2] {'col'}, dimensions={0}, use_global_device_ids=true | all-gather | bytes 589824 | tf_op jit(solution)/shard_map/all_gather | solution.py:275
  63.5 48.0 %shard_map.231 = (bf16[128,1024,128]{2,1,0:T(8,128)(2,1)}, f32[12,72,1024]{2,1,0:T(8,128)}, f32[12,56,128]{2,1,0:T(8,128)}, f32[16,128]{1,0:T(8,128)}) custom-call(bf16[128,1024,128]{2,1,0:T(8,128)(2,1)} %pair.3, f32[12,128,1024]{2,1,0:T(8,128)} %get-tuple-element.18.e_in, f32[12,128,1024]{2,1,0:T(8,128)} %get-tuple-element.19.d_in, ...), custom_call_target="tpu_custom_call" | custom-call | tf_op jit(solution)/shard_map/pallas_call | solution.py:279
  111.6 1.9 copy.96
  113.5 5.0 %copy.98 = f32[864,1024]{0,1:T(8,128)} copy(f32[864,1024]{1,0:T(8,128)} %bitcast.94) | data formatting | bytes 7077888
  118.6 0.9 copy-done.1
  120.1 39.7 %psum.7 = f32[1548]{0:T(1024)S(1)} all-reduce(f32[1548]{0:T(1024)S(1)} %pad_maximum_fusion), channel_id=1, replica_groups=mesh['row'=16,'col'=2] {'row','col'}, use_global_device_ids=true, to_apply=%region_21.22 | all-reduce | flops 1548 | bytes 12384 | tf_op jit(solution)/shard_map/psum | solution.py:325
  161.2 0.9 constant_dynamic-slice_fusion.2
  162.1 1.0 constant_dynamic-slice_fusion.1
  163.7 1.1 copy.97
  165.1 0.7 copy.92
  166.0 34.0 %reduce-scatter.9.cloned.1.call-done = f32[64,864]{1,0:T(8,128)} async-done(((f32[1024,864]{1,0:T(8,128)}), f32[64,864]{1,0:T(8,128)}) %reduce-scatter.9.cloned.1.call-update) | async-done | bytes 221200
  200.0 1.1 copy.99
  201.6 0.7 copy.93
  202.3 0.7 copy.94
  203.0 0.8 multiply_reduce_fusion.4
  203.8 0.8 multiply_reduce_fusion.7
  (101 shorter events, 10.4 us)
Async XLA Ops:
  7.2 0.9 copy-start
  7.2 156.5 %reduce-scatter.7.cloned.1.call-start = ((), (), s32[]{:S(2)}) async-start(), calls=%async_computation.2 | async-start | bytes 589824
  10.5 0.9 copy-start.7
  10.5 1.0 copy-start.12
  10.6 1.0 copy-start.8
  10.6 1.4 copy-start.2
  12.2 0.9 copy-start.5
  12.2 1.7 copy-start.6
  12.2 1.9 copy-start.10
  13.1 3.2 %copy-start.3 = (f32[192,1024]{1,0:T(8,128)S(1)}, f32[192,1024]{1,0:T(8,128)}, u32[]{:S(2)}) copy-start(f32[192,1024]{1,0:T(8,128)} %param.19) | copy-start | bytes 2359300
  16.6 1.4 copy-start.4
  18.1 1.7 copy-start.9
  113.5 86.5 %reduce-scatter.9.cloned.1.call-start = ((), (), s32[]{:S(2)}) async-start(), calls=%async_computation.3 | async-start | bytes 3899392
  118.5 1.0 copy-start.1
  118.5 1.1 copy-start.11
Sparse Core Ops, SparseCore 0:
  113.6 13.5 reduce-scatter.6
  131.0 68.9 reduce-scatter.8

commit v2 on v1

--- a/solution.py
+++ b/solution.py
@@ -67,9 +67,7 @@
     rows = pl.ds(pl.multiple_of(step * block, block), block)
     valid = lax.broadcasted_iota(jnp.int32, (block, cols), 1) < limit_ref[0]
     lane = lax.broadcasted_iota(jnp.int32, (block, 128), 1)
-    peaks = jnp.zeros((block, 128), F32)
-    totals = jnp.ones((block, 128), F32)
-    uppers = jnp.zeros((block, 128), F32)
+    packed = jnp.ones((block, 128), F32)
     for h in range(heads):
         logit = lbase[h, rows, :] + scale * rows_buf[:, h, :]
         logit = jnp.where(valid, logit, F32(-1000000000.0))
@@ -78,75 +76,136 @@
         d = dbase[h, rows, :] + rows_buf[:, PAD + h, :]
         e_out[h] = e
         d_out[h] = d
-        peaks = jnp.where(lane == h, peak, peaks)
-        totals = jnp.where(lane == h, jnp.sum(e, axis=1, keepdims=True), totals)
-        uppers = jnp.where(lane == h, jnp.sum(e * d, axis=1, keepdims=True), uppers)
-    stat_out[0] = peaks
-    stat_out[1] = totals
-    stat_out[2] = uppers
-
-
-def backward_kernel(
-    heads, block, nq, nv, vwidth, pair, e_in, d_in, stats, own, w_hi, w_lo, gpair, qcat, kcat,
-    gcat, vcat, pg_out, key_out, query_out, w_out, rows_buf, att_all, dl_all,
+        packed = jnp.where(lane == h, peak, packed)
+        packed = jnp.where(lane == PAD + h, jnp.sum(e, axis=1, keepdims=True), packed)
+        packed = jnp.where(lane == 2 * PAD + h, jnp.sum(e * d, axis=1, keepdims=True), packed)
+    stat_out[...] = packed
+
+
+def merged(stats, own):
+    peers = stats.shape[0]
+    top = stats[0]
+    for c in range(1, peers):
+        top = jnp.maximum(top, stats[c])
+    total = jnp.zeros_like(top)
+    upper = jnp.zeros_like(top)
+    for c in range(peers):
+        f = jnp.exp(stats[c] - top)
+        total = total + pltpu.roll(stats[c], 128 - PAD, 1) * f
+        upper = upper + pltpu.roll(stats[c], 128 - 2 * PAD, 1) * f
+    return jnp.exp(own - top) / total, upper / total
+
+
+def sums_kernel(
+    nq, nv, vwidth, e_in, d_in, stats, own, qcat, kcat, gcat, vcat, key_out, query_out
 ):
-    step = pl.program_id(0)
-    rows = pl.ds(pl.multiple_of(step * block, block), block)
-
-    @pl.when(step == 0)
+    h = pl.program_id(0)
+    factor, delta = merged(stats, own[...])
+    mine = lax.broadcasted_iota(jnp.int32, factor.shape, 1) == h
+    pick = lambda x: jnp.sum(jnp.where(mine, x, 0.0), axis=1, keepdims=True)
+    att = e_in[0] * pick(factor)
+    dl = att * (d_in[0] - pick(delta))
+    a0, a1 = split2(att)
+    d0, d1 = split2(dl)
+    q = jnp.concatenate(split2(qcat[0]), 0)
+    k = jnp.concatenate(split2(kcat[0]), 0)
+    g = jnp.concatenate(split2(gcat[0]), 0)
+    v = jnp.concatenate(split2(vcat[0]), 0)
+    kk = dot(q, d0, NN) + dot(q, d1, NN)
+    key_out[0, :nq, :] = kk[:nq] + kk[nq:]
+    vv = dot(g, a0, NN) + dot(g, a1, NN)
+    half = g.shape[0] // 2
+    key_out[0, nq:, :] = vv[:nv] + vv[half : half + nv]
+    qq = dot(k, d0, NT) + dot(k, d1, NT)
+    query_out[0, :nq, :] = qq[:nq] + qq[nq:]
+    oo = dot(v, a0, NT) + dot(v, a1, NT)
+    query_out[0, nq:, :] = oo[vwidth:nv] + oo[half + vwidth : half + nv]
+
+
+def pair_kernel(
+    heads, block, pair, e_in, d_in, stats, own, scaled, gpair, pg_out, w_out, rows_buf
+):
+    @pl.when(pl.program_id(0) == 0)
     def _():
         rows_buf[...] = jnp.zeros_like(rows_buf)
         w_out[...] = jnp.zeros_like(w_out)
 
-    peers = stats.shape[0]
-    top = stats[0, 0]
-    for c in range(1, peers):
-        top = jnp.maximum(top, stats[c, 0])
-    total = jnp.zeros_like(top)
-    upper = jnp.zeros_like(top)
-    for c in range(peers):
-        f = jnp.exp(stats[c, 0] - top)
-        total = total + stats[c, 1] * f
-        upper = upper + stats[c, 2] * f
-    factor = jnp.exp(own[0] - top) / total
-    delta = upper / total
+    factor, delta = merged(stats, own[...])
+    w_hi, w_lo = split2(scaled[...])
     for h in range(heads):
         att = e_in[h] * factor[:, h : h + 1]
-        dl = att * (d_in[h] - delta[:, h : h + 1])
-        att_all[h, rows, :] = att
-        dl_all[h, rows, :] = dl
-        rows_buf[:, h, :] = dl
+        rows_buf[:, h, :] = att * (d_in[h] - delta[:, h : h + 1])
         rows_buf[:, PAD + h, :] = att
     acc = w_out[...]
     for r in range(block):
         a = rows_buf[r].astype(BF16)
         lhs = jnp.concatenate([a, a[:PAD]], 0)
-        rhs = jnp.concatenate([w_hi[...], gpair[r], w_lo[...]], 0)
+        rhs = jnp.concatenate([w_hi, gpair[r], w_lo], 0)
         pg_out[r] = dot(lhs, rhs, TN).astype(BF16)
         acc = acc + dot(a[:PAD], pair[r], NN)
     w_out[...] = acc
 
-    @pl.when(step == pl.num_programs(0) - 1)
-    def _():
-        def head(h, carry):
-            d0, d1 = split2(dl_all[h])
-            a0, a1 = split2(att_all[h])
-            q = jnp.concatenate(split2(qcat[h]), 0)
-            k = jnp.concatenate(split2(kcat[h]), 0)
-            g = jnp.concatenate(split2(gcat[h]), 0)
-            v = jnp.concatenate(split2(vcat[h]), 0)
-            kk = dot(q, d0, NN) + dot(q, d1, NN)
-            key_out[h, :nq, :] = kk[:nq] + kk[nq:]
-            vv = dot(g, a0, NN) + dot(g, a1, NN)
-            half = g.shape[0] // 2
-            key_out[h, nq:, :] = vv[:nv] + vv[half : half + nv]
-            qq = dot(k, d0, NT) + dot(k, d1, NT)
-            query_out[h, :nq, :] = qq[:nq] + qq[nq:]
-            oo = dot(v, a0, NT) + dot(v, a1, NT)
-            query_out[h, nq:, :] = oo[vwidth:nv] + oo[half + vwidth : half + nv]
-            return carry
-
-        lax.fori_loop(0, heads, head, 0)
+
+def push_kernel(axes, sizes, total, x, out, slots, send, recv):
+    count = math.prod(sizes)
+    place = 0
+    for axis, size in zip(axes, sizes):
+        place = place * size + lax.axis_index(axis)
+    copies = []
+    for step in range(1, count):
+        peer = lax.rem(place + step, count)
+        device = {}
+        rest = peer
+        for axis, size in reversed(list(zip(axes, sizes))):
+            device[axis] = lax.rem(rest, size)
+            rest = rest // size
+        copy = pltpu.make_async_remote_copy(
+            src_ref=x,
+            dst_ref=slots.at[place],
+            send_sem=send.at[step],
+            recv_sem=recv.at[place],
+            device_id=device,
+            device_id_type=pl.DeviceIdType.MESH,
+        )
+        copy.start()
+        copies.append(copy)
+    slots[place] = x[...]
+    for step in range(1, count):
+        source = lax.rem(place + step, count)
+        pltpu.make_async_remote_copy(
+            src_ref=x,
+            dst_ref=slots.at[source],
+            send_sem=send.at[step],
+            recv_sem=recv.at[source],
+            device_id=device,
+            device_id_type=pl.DeviceIdType.MESH,
+        ).wait_recv()
+    for copy in copies:
+        copy.wait_send()
+    if total:
+        acc = slots[0]
+        for c in range(1, count):
+            acc = acc + slots[c]
+        out[...] = acc
+    else:
+        out[...] = slots[...]
+
+
+def pushed(x, axes, total):
+    sizes = tuple(lax.axis_size(axis) for axis in axes)
+    count = math.prod(sizes)
+    return pl.pallas_call(
+        functools.partial(push_kernel, axes, sizes, total),
+        in_specs=[pl.BlockSpec(memory_space=pltpu.VMEM)],
+        out_specs=pl.BlockSpec(memory_space=pltpu.VMEM),
+        out_shape=jax.ShapeDtypeStruct(x.shape if total else (count, *x.shape), F32),
+        scratch_shapes=[
+            pltpu.VMEM((count, *x.shape), F32),
+            pltpu.SemaphoreType.DMA((count,)),
+            pltpu.SemaphoreType.DMA((count,)),
+        ],
+        compiler_params=pltpu.CompilerParams(has_side_effects=True),
+    )(x)
 
 
 def turn(rotation, local):
@@ -231,7 +290,6 @@
     vcat = pad_rows(jnp.concatenate([values.reshape(heads, width, n_cols), vg], axis=1), nvp)
     w_t = jnp.pad(bias_weight.T, ((0, PAD - heads), (0, 0)))
     scaled = logit_scale * w_t.astype(F32)
-    w_hi, w_lo = split2(scaled)
     gpair = pad_rows(grad_pair, PAD)
     limit = residue_count - col_start
 
@@ -241,7 +299,7 @@
     pair_spec = pl.BlockSpec((block, n_cols, channels), lambda i: (i, 0, 0))
     gpair_spec = pl.BlockSpec((block, PAD, channels), lambda i: (i, 0, 0))
     hij_spec = pl.BlockSpec((heads, block, n_cols), lambda i: (0, i, 0))
-    stat_spec = pl.BlockSpec((3, block, 128), lambda i: (0, i, 0))
+    stat_spec = pl.BlockSpec((block, 128), lambda i: (i, 0))
     cat_specs = [
         whole(heads, nq, n_rows),
         whole(heads, nq, n_cols),
@@ -263,7 +321,7 @@
             *cat_specs,
         ],
         out_specs=[hij_spec, hij_spec, stat_spec],
-        out_shape=[hij, hij, jax.ShapeDtypeStruct((3, n_rows, 128), F32)],
+        out_shape=[hij, hij, jax.ShapeDtypeStruct((n_rows, 128), F32)],
         scratch_shapes=[
             pltpu.VMEM((heads, n_rows, n_cols), F32),
             pltpu.VMEM((heads, n_rows, n_cols), F32),
@@ -272,62 +330,73 @@
         compiler_params=params,
     )(limit, pair_rep, w_t, gpair, qcat, kcat, gcat, vcat)
 
-    stats = lax.all_gather(own, "col")
+    stats = pushed(own, ("col",), False)
     peers = stats.shape[0]
     nk = nq + nv
     nr = nq + nv - width
-    pair_grad, key_out, query_out, w_out = pl.pallas_call(
-        functools.partial(backward_kernel, heads, block, nq, nv, width),
-        grid=grid,
+    per_head = lambda *shape: pl.BlockSpec((1, *shape), lambda i: (i, 0, 0))
+    key_out, query_out = pl.pallas_call(
+        functools.partial(sums_kernel, nq, nv, width),
+        grid=(heads,),
         in_specs=[
-            pair_spec,
-            hij_spec,
-            hij_spec,
-            pl.BlockSpec((peers, 3, block, 128), lambda i: (0, 0, i, 0)),
-            stat_spec,
-            whole(PAD, channels),
-            whole(PAD, channels),
-            gpair_spec,
-            *cat_specs,
-        ],
-        out_specs=[
-            pair_spec,
-            whole(heads, nk, n_cols),
-            whole(heads, nr, n_rows),
-            whole(PAD, channels),
-        ],
+            per_head(n_rows, n_cols),
+            per_head(n_rows, n_cols),
+            whole(peers, n_rows, 128),
+            whole(n_rows, 128),
+            per_head(nq, n_rows),
+            per_head(nq, n_cols),
+            per_head(nvp, n_rows),
+            per_head(nvp, n_cols),
+        ],
+        out_specs=[per_head(nk, n_cols), per_head(nr, n_rows)],
         out_shape=[
-            jax.ShapeDtypeStruct(pair_rep.shape, BF16),
             jax.ShapeDtypeStruct((heads, nk, n_cols), F32),
             jax.ShapeDtypeStruct((heads, nr, n_rows), F32),
-            jax.ShapeDtypeStruct((PAD, channels), F32),
-        ],
-        scratch_shapes=[
-            pltpu.VMEM((block, 2 * PAD, n_cols), F32),
-            pltpu.VMEM((heads, n_rows, n_cols), F32),
-            pltpu.VMEM((heads, n_rows, n_cols), F32),
         ],
         compiler_params=params,
-    )(pair_rep, e_all, d_all, stats, own, w_hi, w_lo, gpair, qcat, kcat, gcat, vcat)
-
-    distance_part = jnp.sum(
-        q_square[:, 0] * query_out[:, qsize + 1] + query_out[:, qsize], axis=1
-    ) - 2.0 * jnp.sum(qg * query_out[:, width:qsize], axis=(1, 2))
-    weight_part = logit_scale * w_out[:heads].T
-    small = jnp.concatenate([weight_part.reshape(-1), distance_part])
-
+    )(e_all, d_all, stats, own, qcat, kcat, gcat, vcat)
     key_sum = lax.psum_scatter(
         key_out.reshape(heads * nk, n_cols), "row", scatter_dimension=1, tiled=True
     ).reshape(heads, nk, -1)
     query_sum = lax.psum_scatter(
         query_out.reshape(heads * nr, n_rows), "col", scatter_dimension=1, tiled=True
     ).reshape(heads, nr, -1)
-    small = lax.psum(small, ("row", "col"))
-    weight_total = small[: channels * heads].reshape(channels, heads)
+    pair_grad, w_out = pl.pallas_call(
+        functools.partial(pair_kernel, heads, block),
+        grid=grid,
+        in_specs=[
+            pair_spec,
+            hij_spec,
+            hij_spec,
+            pl.BlockSpec((peers, block, 128), lambda i: (0, i, 0)),
+            stat_spec,
+            whole(PAD, channels),
+            gpair_spec,
+        ],
+        out_specs=[pair_spec, whole(PAD, channels)],
+        out_shape=[
+            jax.ShapeDtypeStruct(pair_rep.shape, BF16),
+            jax.ShapeDtypeStruct((PAD, channels), F32),
+        ],
+        scratch_shapes=[pltpu.VMEM((block, 2 * PAD, n_cols), F32)],
+        compiler_params=params,
+        cost_estimate=pl.CostEstimate(
+            flops=8 * n_rows * n_cols * channels * PAD,
+            bytes_accessed=4 * n_rows * n_cols * channels + 8 * heads * n_rows * n_cols,
+            transcendentals=0,
+        ),
+    )(pair_rep, e_all, d_all, stats, own, scaled, gpair)
+
+    distance_part = jnp.sum(
+        q_square[:, 0] * query_out[:, qsize + 1] + query_out[:, qsize], axis=1
+    ) - 2.0 * jnp.sum(qg * query_out[:, width:qsize], axis=(1, 2))
+    small = jnp.concatenate(
+        [logit_scale * w_out, jnp.pad(distance_part, (0, 8 * channels - heads)).reshape(8, channels)]
+    )
+    small = pushed(small, ("row", "col"), True)
+    weight_total = small[:heads].T
     head_weight_grad = (
-        small[channels * heads :]
-        * (-0.5 * logit_scale * point_scale)
-        * jax.nn.sigmoid(head_weight)
+        small[PAD, :heads] * (-0.5 * logit_scale * point_scale) * jax.nn.sigmoid(head_weight)
     )
 
     share = query_sum.shape[2]

time: 214 us -> 195 us (0.911)
  blocking collectives: 50.8 us -> 0 us
  Pallas kernels: 79.1 us -> 117 us
  waiting for transfers between devices: 34 us -> 19.3 us
  other arithmetic: 10.5 us -> 17.1 us
    psum x1 -> x0, blocking collectives: 39.7 us -> none  [per_device(): small = lax.psum(small, ('row', 'col'))]
    pallas_call x1 -> x4, Pallas kernels: 48 us -> 86.1 us  [the longest x1 38.6 us: per_device(): pl.pallas_call(functools.partial(pair_kernel, heads, block), grid=grid, i...]
    unnamed x4, waiting for transfers between devices: 34 us -> 19.3 us
    all_gather x1 -> x0, blocking collectives: 11.1 us -> none  [per_device(): stats = lax.all_gather(own, 'col')]
    unnamed x37 -> x42, local copies, waits for them, and re-layouts: 14.8 us -> 14.7 us
  transfers between devices with their start and end apart: 2 -> 2, of which waited for: 1 -> 1; matrix products, arithmetic and copies ran while one was open for 5% -> 8% of each run, Pallas kernels for 0% -> 30%
where the time goes in v2:
time: 195 us; the launch traced here: 193 us
  Pallas kernels  117 us (60%)
  local copies, waits for them, and re-layouts  24.1 us (12%)
  waiting for transfers between devices  19.3 us (10%)
  other arithmetic  17.1 us (9%)
  between operations  15.2 us (8%)
    pallas_call x1, Pallas kernels, per_device(): pl.pallas_call(functools.partial(pair_kernel, heads, block), grid=grid, i...  38.6 us
    pallas_call x2, Pallas kernels, pushed(): pl.pallas_call(functools.partial(push_kernel, axes, sizes, total), in_spe...  32 us
    pallas_call x1, Pallas kernels, per_device(): pl.pallas_call(functools.partial(forward_kernel, heads, block, logit_scal...  31.1 us
    unnamed x4, waiting for transfers between devices  19.3 us
    pallas_call x1, Pallas kernels, per_device(): pl.pallas_call(functools.partial(sums_kernel, nq, nv, width), grid=(heads...  15.5 us
    unnamed x42, local copies, waits for them, and re-layouts  14.7 us
  transfers between devices with their start and end apart: 2, of which 1 were waited for; matrix products, arithmetic and copies ran while one was open for 8% of the time, Pallas kernels for 30%

profile of v2, /device:TPU:0, one launch (start us, length us, event | category | flops | bytes accessed | tf_op | source)
XLA Modules:
  0.0 193.0 jit_solution(15438477673631403946)
XLA Ops:
  10.1 1.2 broadcast_multiply_fusion.3
  11.8 0.9 multiply_reduce_fusion.11
  12.8 1.6 broadcast_multiply_fusion.1
  14.4 1.0 multiply_reduce_fusion.3
  16.9 0.9 pad.29.gpair
  18.8 1.0 copy-done.2
  21.7 1.7 select_maximum_fusion.vcat
  23.7 1.3 pad.31.kcat
  25.7 31.1 %shard_map.230 = (f32[12,128,1024]{2,1,0:T(8,128)}, f32[12,128,1024]{2,1,0:T(8,128)}, f32[128,128]{1,0:T(8,128)}) custom-call(s32[1]{0:T(128)S(6)} %sub.25.limit_ref, bf16[128,1024,128]{2,1,0:T(8,128)(2,1)} %pair.3, bf16[16,128]{1,0:T(8,128)(2,1)} %pad.28.bias_w, bf16[128,16,128]{2,1,0:T(8,128)(2,1)} %pad.29.gpair, ...), custom_call_target="tpu_custom_call" | custom-call | tf_op jit(solution)/shard_map/pallas_call | solution.py:313
  56.8 13.0 %shard_map.231.stats = f32[2,128,128]{2,1,0:T(8,128)} custom-call(f32[128,128]{1,0:T(8,128)} %get-tuple-element.20.x.own), custom_call_target="tpu_custom_call" | custom-call | tf_op jit(solution)/shard_map/pallas_call | solution.py:197
  69.8 15.5 %shard_map.233 = (f32[12,72,1024]{2,1,0:T(8,128)}, f32[12,56,128]{2,1,0:T(8,128)}) custom-call(f32[12,128,1024]{2,1,0:T(8,128)} %get-tuple-element.18.e_in, f32[12,128,1024]{2,1,0:T(8,128)} %get-tuple-element.19.d_in, f32[2,128,128]{2,1,0:T(8,128)} %shard_map.231.stats, f32[128,128]{1,0:T(8,128)} %get-tuple-element.20.x.own, ...), custom_call_target="tpu_custom_call" | custom-call | tf_op jit(solution)/shard_map/pallas_call | solution.py:338
  85.3 1.9 copy.90
  87.3 5.0 %copy.92 = f32[864,1024]{0,1:T(8,128)} copy(f32[864,1024]{1,0:T(8,128)} %bitcast.96) | data formatting | bytes 7077888
  92.3 0.9 copy-done.1
  93.3 0.8 copy.85
  94.6 0.8 fusion.3
  96.2 38.6 %shard_map.232 = (bf16[128,1024,128]{2,1,0:T(8,128)(2,1)}, f32[16,128]{1,0:T(8,128)}) custom-call(bf16[128,1024,128]{2,1,0:T(8,128)(2,1)} %pair.3, f32[12,128,1024]{2,1,0:T(8,128)} %get-tuple-element.18.e_in, f32[12,128,1024]{2,1,0:T(8,128)} %get-tuple-element.19.d_in, f32[2,128,128]{2,1,0:T(8,128)} %shard_map.231.stats, ...), custom_call_target="tpu_custom_call" | custom-call | flops 2147483648 | bytes 79691776 | tf_op jit(solution)/shard_map/pallas_call | solution.py:364
  136.2 19.0 %shard_map.234 = f32[24,128]{1,0:T(8,128)} custom-call(f32[24,128]{1,0:T(8,128)} %pad_maximum_fusion.x), custom_call_target="tpu_custom_call" | custom-call | tf_op jit(solution)/shard_map/pallas_call | solution.py:197
  155.3 0.9 constant_dynamic-slice_fusion.2
  156.3 1.2 divide_multiply_fusion
  157.5 1.3 slice_bitcast_fusion.4
  158.8 1.1 copy.91
  161.2 19.2 %reduce-scatter.9.cloned.1.call-done = f32[64,864]{1,0:T(8,128)} async-done(((f32[1024,864]{1,0:T(8,128)}), f32[64,864]{1,0:T(8,128)}) %reduce-scatter.9.cloned.1.call-update) | async-done | bytes 221200
  180.4 1.1 copy.93
  (106 shorter events, 16.9 us)
Async XLA Ops:
  7.2 0.8 copy-start
  7.2 8.9 %copy-start.8 = (bf16[128,12,128]{2,0,1:T(8,128)(2,1)S(1)}, bf16[128,12,128]{2,0,1:T(8,128)(2,1)}, u32[]{:S(2)}) copy-start(bf16[128,12,128]{2,0,1:T(8,128)(2,1)} %param.29) | copy-start | bytes 1179652
  7.2 9.1 %copy-start.12 = (bf16[128,12]{0,1:T(8,128)(2,1)S(1)}, bf16[128,12]{0,1:T(8,128)(2,1)}, u32[]{:S(2)}) copy-start(bf16[128,12]{0,1:T(8,128)(2,1)} %param.16) | copy-start | bytes 9220
  7.2 151.6 %reduce-scatter.7.cloned.1.call-start = ((), (), s32[]{:S(2)}) async-start(), calls=%async_computation.2 | async-start | bytes 589824
  12.8 5.1 %copy-start.5 = (f32[3,48,1024]{2,1,0:T(8,128)S(1)}, f32[3,48,1024]{2,1,0:T(8,128)}, u32[]{:S(2)}) copy-start(f32[3,48,1024]{2,1,0:T(8,128)} %param.22) | copy-start | bytes 1769476
  18.4 1.3 copy-start.2
  20.0 0.7 copy-start.14
  20.0 0.9 copy-start.7
  20.0 1.0 copy-start.11
  20.0 1.7 copy-start.4
  21.7 1.7 copy-start.3
  23.7 1.4 copy-start.9
  87.3 93.2 %reduce-scatter.9.cloned.1.call-start = ((), (), s32[]{:S(2)}) async-start(), calls=%async_computation.3 | async-start | bytes 3899392
  92.3 1.0 copy-start.1
  92.3 1.8 copy-start.6
  96.2 59.9 %copy-start.10 = (f32[3,48,128]{2,1,0:T(8,128)S(1)}, f32[3,48,128]{2,1,0:T(8,128)}, u32[]{:S(2)}) copy-start(f32[3,48,128]{2,1,0:T(8,128)} %param.21) | copy-start | bytes 221188
  96.2 60.1 %copy-start.15 = (f32[12]{0:T(128)S(1)}, f32[12]{0:T(128)}, u32[]{:S(2)}) copy-start(f32[12]{0:T(128)} %param.17) | copy-start | bytes 148
  96.2 63.7 %copy-start.13 = (f32[12]{0:T(128)S(1)}, f32[12]{0:T(128)}, u32[]{:S(2)}) copy-start(f32[12]{0:T(128)} %get-tuple-element.75) | copy-start | bytes 148
Sparse Core Ops, SparseCore 0:
  87.4 13.2 reduce-scatter.6
  104.5 75.8 reduce-scatter.8
